TPU v7x, 16 devices: a whole 2x2x2 slice. The times are simulated.
16 devices in a mesh: dp: 1, ep: 16 (over x, y, z, core).
Axes of the slice: x: 2, y: 2, z: 2, core: 2. Of those that a mesh axis runs over, the one named last changes fastest.
Arguments:
- x: bfloat16 [1, 16, 256, 2560], P('dp', 'ep')
- expert: int32 [1, 16, 256, 6], P('dp', 'ep')
- slot: int32 [1, 16, 256, 6], P('dp', 'ep')
- gate: float32 [1, 16, 256, 6], P('dp', 'ep')
- w_gate: bfloat16 [80, 2560, 1536], P('ep')
- w_up: bfloat16 [80, 2560, 1536], P('ep')
- w_down: bfloat16 [80, 1536, 2560], P('ep')
- s_gate: bfloat16 [2560, 3072], replicated
- s_up: bfloat16 [2560, 3072], replicated
- s_down: bfloat16 [3072, 2560], replicated
Outputs:
- y: bfloat16 [1, 16, 256, 2560], P('dp', 'ep')
All inputs are finite; a program needn't handle non-finite values.
Results may differ from a plain program's by a relative error of at most 0.009.
Values are sent between devices in bfloat16 or wider.
A program may use at most 2 GiB of HBM per device.

v0:
```python
import jax
import jax.numpy as jnp
from jax import lax
from jax.sharding import NamedSharding, PartitionSpec as P


def einsum(form, a, b):
    return jnp.einsum(form, a.astype(jnp.float32), b.astype(jnp.float32))


def for_all(x, s_gate, s_up, s_down):
    h = jax.nn.silu(einsum("...d,df->...f", x, s_gate)) * einsum("...d,df->...f", x, s_up)
    return einsum("...f,fd->...d", h.astype(jnp.bfloat16), s_down)


def solution(mesh):
    def placed(v, *spec):
        return lax.with_sharding_constraint(v, NamedSharding(mesh, P(*spec)))

    def step(x, expert, slot, gate, w_gate, w_up, w_down, s_gate, s_up, s_down):
        experts, (tokens, top) = w_gate.shape[0], expert.shape[2:]
        slots = 5 * tokens * top // (4 * experts)
        to_expert = jax.nn.one_hot(expert, experts, dtype=jnp.bfloat16)
        to_slot = jax.nn.one_hot(slot, slots, dtype=jnp.bfloat16)
        weighted = to_expert * gate[..., None].astype(jnp.bfloat16)
        dispatch = einsum("abtke,abtkc->abtec", to_expert, to_slot).astype(jnp.bfloat16)
        combine = einsum("abtke,abtkc->abtec", weighted, to_slot).astype(jnp.bfloat16)
        z = einsum("abtec,abtd->aebcd", dispatch, x).astype(jnp.bfloat16)
        z = placed(z, "dp", None, "ep", None, None)
        z = placed(z, "dp", "ep", None, None, None)
        h = jax.nn.silu(einsum("aebcd,edf->aebcf", z, w_gate))
        h = (h * einsum("aebcd,edf->aebcf", z, w_up)).astype(jnp.bfloat16)
        out = einsum("aebcf,efd->aebcd", h, w_down).astype(jnp.bfloat16)
        out = placed(out, "dp", "ep", None, None, None)
        out = placed(out, "dp", None, "ep", None, None)
        y = einsum("abtec,aebcd->abtd", combine, out)
        return (y + for_all(x, s_gate, s_up, s_down)).astype(jnp.bfloat16)

    return step
```

profile of v0, /device:TPU:0, one launch (start us, length us, event | category | flops | bytes accessed | tf_op | source)
XLA Modules:
  0.0 392.7 jit_solution(16184683611306030281)
XLA Ops:
  0.0 0.0 copy-start
  0.0 0.9 copy.25
  0.9 0.0 copy-start.1
  0.9 0.8 copy.27
  1.8 0.0 copy-start.3
  1.8 0.0 copy-done.1
  1.8 0.6 copy-done.3
  2.5 3.6 convolution_convert_fusion.1
  6.1 2.4 copy.13
  8.6 0.0 copy-done
  8.6 3.0 convolution_convert_fusion
  11.6 115.4 %all-to-all.4 = bf16[1,16,5,1,24,2560]{5,4,2,3,0,1:T(8,128)(2,1)} all-to-all(bf16[1,16,5,1,24,2560]{5,4,2,3,0,1:T(8,128)(2,1)S(1)} %bitcast.127), channel_id=1, replica_groups=mesh['dp'=1,'ep'=16] {'ep'}, dimensions={1} | all-to-all | bytes 19660800 | tf_op jit(solution)/sharding_constraint;jit(solution)/sharding_constraint | solution.py:18
  127.0 29.9 %fusion.2 = f32[5,16,24,1536]{3,2,1,0:T(8,128)} fusion(bf16[5,2560,1536]{2,1,0:T(8,128)(2,1)} %param.5, bf16[1,16,5,1,24,2560]{5,4,2,3,0,1:T(8,128)(2,1)} %all-to-all.4), kind=kOutput, calls=%fused_computation.2 | convolution fusion | flops 15099494400 | bytes 60948480 | tf_op jit(solution)/aebcd,edf->aebcf/dot_general | solution.py:8
  156.8 30.1 %fusion.4 = f32[5,16,24,1536]{3,2,1,0:T(8,128)} fusion(bf16[5,2560,1536]{2,1,0:T(8,128)(2,1)} %param.4, bf16[1,16,5,1,24,2560]{5,4,2,3,0,1:T(8,128)(2,1)} %all-to-all.4), kind=kOutput, calls=%fused_computation.4 | convolution fusion | flops 15099494400 | bytes 60948480 | tf_op jit(solution)/aebcd,edf->aebcf/dot_general | solution.py:8
  187.0 28.3 %convert_bitcast_fusion = bf16[1,5,16,1,24,2560]{5,4,2,1,3,0:T(8,128)(2,1)} fusion(bf16[5,1536,2560]{2,1,0:T(8,128)(2,1)} %param.6, f32[5,16,24,1536]{3,2,1,0:T(8,128)} %fusion.2, f32[5,16,24,1536]{3,2,1,0:T(8,128)} %fusion.4), kind=kOutput, calls=%fused_computation.15 | convolution fusion | flops 15122104320 | bytes 72744960 | tf_op jit(solution)/aebcf,efd->aebcd/dot_general | solution.py:8
  215.3 8.2 %copy.16 = bf16[1,5,16,1,24,2560]{5,4,1,3,0,2:T(8,128)(2,1)} copy(bf16[1,5,16,1,24,2560]{5,4,2,1,3,0:T(8,128)(2,1)} %convert_bitcast_fusion) | data formatting | bytes 19660800 | tf_op jit(solution)/sharding_constraint;jit(solution)/sharding_constraint | solution.py:18
  223.5 0.0 copy-start.5
  223.5 0.0 copy-start.2
  223.5 0.0 copy-start.4
  223.5 3.9 all-to-all-start.1
  227.4 0.0 copy-done.5
  227.4 0.1 copy.26
  227.6 0.0 copy-done.2
  227.6 0.0 copy-done.4
  227.6 3.9 convolution_convert_fusion.2
  231.5 2.4 copy.23
  233.9 7.7 %convolution_bitcast_fusion.1 = f32[1,256,3072]{2,1,0:T(8,128)S(1)} fusion(bf16[2560,3072]{1,0:T(8,128)(2,1)} %param.7, bf16[1,1,256,2560]{3,2,1,0:T(8,128)(2,1)S(1)} %copy-done), kind=kOutput, calls=%fused_computation.21 | convolution fusion | flops 4026531840 | bytes 20185088 | tf_op jit(solution)/...d,df->...f/dot_general | solution.py:8
  241.6 11.3 %fusion.21 = bf16[256,3072]{1,0:T(8,128)(2,1)} fusion(bf16[2560,3072]{1,0:T(8,128)(2,1)} %param.8, f32[1,256,3072]{2,1,0:T(8,128)S(1)} %convolution_bitcast_fusion.1, bf16[1,1,256,2560]{3,2,1,0:T(8,128)(2,1)S(1)} %copy-done), kind=kOutput, calls=%fused_computation.27 | convolution fusion | flops 4031250432 | bytes 21757952 | tf_op jit(solution)/...d,df->...f/dot_general | solution.py:8
  252.9 125.0 %all-to-all-done.1 = bf16[1,5,16,1,24,2560]{5,4,1,3,0,2:T(8,128)(2,1)} async-done(((bf16[1,5,16,1,24,2560]{5,4,1,3,0,2:T(8,128)(2,1)}), bf16[1,5,16,1,24,2560]{5,4,1,3,0,2:T(8,128)(2,1)}, u32[]{:S(2)}, u32[]{:S(2)}) %all-to-all-start.1) | async-done | bytes 9830432 | tf_op jit(solution)/sharding_constraint;jit(solution)/sharding_constraint | solution.py:18
  377.9 0.0 copy-start.6
  377.9 5.6 %convolution_bitcast_fusion.2 = f32[256,2560]{1,0:T(8,128)S(1)} fusion(bf16[256,80,24]{0,2,1:T(8,128)(2,1)S(1)} %copy.23, bf16[80,24,2560]{2,1,0:T(8,128)(2,1)} %bitcast.38), kind=kOutput, calls=%fused_computation.23 | convolution fusion | flops 2516582400 | bytes 13434880 | tf_op jit(solution)/abtec,aebcd->abtd/dot_general | solution.py:8
  383.5 0.0 copy-done.6
  383.5 9.1 %fusion.22 = bf16[1,1,256,2560]{3,2,1,0:T(8,128)(2,1)} fusion(f32[256,2560]{1,0:T(8,128)S(1)} %convolution_bitcast_fusion.2, bf16[256,3072]{1,0:T(8,128)(2,1)S(1)} %copy-done.6, bf16[3072,2560]{1,0:T(8,128)(2,1)} %param.9), kind=kOutput, calls=%fused_computation.28 | convolution fusion | flops 4027842560 | bytes 21233664 | tf_op jit(solution)/...f,fd->...d/dot_general | solution.py:8
  (1 shorter events, 0.0 us)
Async XLA Ops:
  0.0 8.6 %copy-start = (bf16[1,1,256,2560]{3,2,1,0:T(8,128)(2,1)S(1)}, bf16[1,1,256,2560]{3,2,1,0:T(8,128)(2,1)}, u32[]{:S(2)}) copy-start(bf16[1,1,256,2560]{3,2,1,0:T(8,128)(2,1)} %param.3) | copy-start | bytes 3932164
  0.9 0.9 copy-start.1
  1.8 0.7 copy-start.3
  223.5 3.9 copy-start.5
  223.5 4.1 %copy-start.2 = (s32[1,1,256,6]{3,2,1,0:T(8,128)S(1)}, s32[1,1,256,6]{3,2,1,0:T(8,128)}, u32[]{:S(2)}) copy-start(s32[1,1,256,6]{3,2,1,0:T(8,128)} %copy-done.1) | copy-start | bytes 18436
  223.5 4.1 %copy-start.4 = (s32[1,1,256,6]{3,2,1,0:T(8,128)S(1)}, s32[1,1,256,6]{3,2,1,0:T(8,128)}, u32[]{:S(2)}) copy-start(s32[1,1,256,6]{3,2,1,0:T(8,128)} %copy-done.3) | copy-start | bytes 18436
  223.5 154.4 %all-to-all-start.1 = ((bf16[1,5,16,1,24,2560]{5,4,1,3,0,2:T(8,128)(2,1)}), bf16[1,5,16,1,24,2560]{5,4,1,3,0,2:T(8,128)(2,1)}, u32[]{:S(2)}, u32[]{:S(2)}) async-start(bf16[1,5,16,1,24,2560]{5,4,1,3,0,2:T(8,128)(2,1)} %copy.16), calls=%async_computation.1 | async-start | bytes 19660800 | tf_op jit(solution)/sharding_constraint;jit(solution)/sharding_constraint | solution.py:18
  377.9 5.7 %copy-start.6 = (bf16[256,3072]{1,0:T(8,128)(2,1)S(1)}, bf16[256,3072]{1,0:T(8,128)(2,1)}, u32[]{:S(2)}) copy-start(bf16[256,3072]{1,0:T(8,128)(2,1)} %fusion.21) | copy-start | bytes 4718596
where the time goes:
time: 393 us
  matrix products  133 us (34%)
  waiting for transfers between devices  125 us (32%)
  blocking collectives  115 us (29%)
  local copies, waits for them, and re-layouts  15.7 us (4%)
    dot_general x10, matrix products, einsum(): return jnp.einsum(form, a.astype(jnp.float32), b.astype(jnp.float32))  133 us
    another operation x1, waiting for transfers between devices, placed(): return lax.with_sharding_constraint(v, NamedSharding(mesh, P(*spec)))  125 us
    another operation x1, blocking collectives, placed(): return lax.with_sharding_constraint(v, NamedSharding(mesh, P(*spec)))  115 us
    another operation x1, local copies, waits for them, and re-layouts, placed(): return lax.with_sharding_constraint(v, NamedSharding(mesh, P(*spec)))  8.24 us
  transfers between devices with their start and end apart: 1, of which 1 were waited for; matrix products, arithmetic and copies ran while one was open for 6% of the time, Pallas kernels for 0%

commit v1 on v0

v1 whole, which is shorter than its diff:
```python
import functools

import jax
import jax.numpy as jnp
from jax import lax
from jax.experimental import pallas as pl
from jax.experimental.pallas import tpu as pltpu
from jax.sharding import PartitionSpec as P

MESH = pl.DeviceIdType.MESH
BF = jnp.bfloat16
F32 = jnp.float32
DC = 256
BITS = (4, 2, 1)
PARTS = ((0, 96), (96, 80), (176, 80))
RING = 4
DROPPED = 128


def axes(me):
    def flip(bit):
        return me + bit * (1 - 2 * lax.rem(lax.div(me, bit), 2))

    return [flip(2 * b) for b in BITS], flip(1)


def meet(links, twin):
    barrier = pltpu.get_barrier_semaphore()
    for other in (*links, twin):
        pl.semaphore_signal(barrier, inc=1, device_id={"ep": other}, device_id_type=MESH)
    pl.semaphore_wait(barrier, 4)


def silu_mul(g, u):
    return (g * jax.nn.sigmoid(g) * u).astype(BF)


def up_kernel(x_ref, m_ref, wg, wu, sg, su, h_out, hs_out, cm_out,
              xr, mr, dm, cm, zs, ag, au, wb, hb, hsb, ss, rs, wsem, osem):
    me = lax.axis_index("ep")
    links, twin = axes(me)
    nc = xr.shape[0]
    experts, rows, ff = ag.shape
    tokens = x_ref.shape[0]
    slots = rows // 16
    n_shared = 2 * nc
    n_steps = n_shared + nc * experts

    def start_w(s):
        slot = lax.rem(s, RING)

        @pl.when(s < n_shared)
        def _():
            half, k = lax.div(s, nc), lax.rem(s, nc)
            at = (pl.ds(pl.multiple_of(k * DC, DC), DC), pl.ds(pl.multiple_of(half * ff, ff), ff))
            for i, w in enumerate((sg, su)):
                pltpu.make_async_copy(w.at[at], wb.at[slot, i], wsem.at[slot, i]).start()

        @pl.when((s >= n_shared) & (s < n_steps))
        def _():
            k, e = lax.div(s - n_shared, experts), lax.rem(s - n_shared, experts)
            for i, w in enumerate((wg, wu)):
                src = w.at[e, pl.ds(pl.multiple_of(k * DC, DC), DC), :]
                pltpu.make_async_copy(src, wb.at[slot, i], wsem.at[slot, i]).start()

    def wait_w(s):
        slot = lax.rem(s, RING)
        for i, w in enumerate((wg, wu)):
            pltpu.make_async_copy(w.at[0, pl.ds(0, DC), :], wb.at[slot, i], wsem.at[slot, i]).wait()
        return slot

    for s in range(RING):
        start_w(s)
    meet(links, twin)

    def copy(kind, i, k):
        row = nc if k is None else k
        own = m_ref if k is None else x_ref.at[:, pl.ds(pl.multiple_of(k * DC, DC), DC)]

        def block(slot):
            return mr.at[slot] if k is None else xr.at[k, slot]

        if kind == "D":
            src, dst, to, n = own, block(2 * BITS[i]), links[i], i
        elif kind == "F":
            src, dst = block(2 * BITS[(i + 1) % 3]), block(2 * (BITS[i] | BITS[(i + 1) % 3]))
            to, n = links[i], 3 + i
        elif kind == "G":
            part = pl.ds(*PARTS[i])
            src = block(2 * (BITS[(i + 1) % 3] | BITS[(i + 2) % 3])).at[part]
            dst, to, n = block(14).at[part], links[i], 6 + i
        else:
            src, dst, to, n = own if i == 0 else block(2 * i), block(2 * i + 1), twin, 9 + i
        return pltpu.make_async_remote_copy(
            src_ref=src, dst_ref=dst, send_sem=ss.at[row, n], recv_sem=rs.at[row, n],
            device_id={"ep": to}, device_id_type=MESH)

    def both(k, do):
        @pl.when(k == 0)
        def _():
            do(None)

        do(k)

    def first(k):
        for i in range(3):
            copy("D", i, k).start()

    def second(k):
        for i in range(3):
            copy("D", i, k).wait_recv()
            copy("F", (i + 2) % 3, k).start()
            copy("S", BITS[i], k).start()

    def third(k):
        for i in range(3):
            copy("F", i, k).wait_recv()
            copy("G", (i + 2) % 3, k).start()
            copy("S", BITS[i] | BITS[(i + 1) % 3], k).start()

    def fourth(k):
        for i in range(3):
            copy("G", i, k).wait_recv()
        copy("S", 7, k).start()

    def arrive(k):
        for q in range(8):
            copy("S", q, k).wait_recv()

    def leave(k):
        for kind, count in (("D", 3), ("F", 3), ("G", 3), ("S", 8)):
            for i in range(count):
                copy(kind, i, k).wait_send()

    first(None)
    for k in range(3):
        first(k)
    copy("S", 0, None).start()

    @pl.loop(0, nc)
    def _(k):
        copy("S", 0, k).start()
        xr[k, 0] = x_ref[:, pl.ds(pl.multiple_of(k * DC, DC), DC)]

    mr[0] = m_ref[...]

    def matmul(lhs, slot, e, m, fresh):
        for n in range(ff // 256):
            cols = slice(256 * n, 256 * (n + 1))
            for i, acc in enumerate((ag, au)):
                old = jnp.where(fresh, 0.0, acc[e, :m, cols])
                acc[e, :m, cols] = old + jnp.dot(lhs, wb[slot, i, :, cols], preferred_element_type=F32)

    def shared_step(s):
        slot = wait_w(s)
        half, k = lax.div(s, nc), lax.rem(s, nc)
        matmul(xr[k, 0], slot, 0, tokens, k == 0)
        start_w(s + RING)

        @pl.when(k == nc - 1)
        def _():
            for n in range(ff // 256):
                cols = slice(256 * n, 256 * (n + 1))
                at = pl.ds(pl.multiple_of(half * ff + 256 * n, 256), 256)
                hsb[:, at] = silu_mul(ag[0, :tokens, cols], au[0, :tokens, cols])

    def masks():
        base = (me * (experts * slots)).astype(F32)
        lane = lax.broadcasted_iota(jnp.int32, (tokens, 128), 1)
        want = jnp.where(lane < experts * slots, lane.astype(F32) + base, -1.0)

        @pl.loop(0, 16)
        def _(d):
            m = mr[d].astype(F32)
            hit = jnp.zeros((tokens, 128), F32)
            weight = jnp.zeros((tokens, 128), F32)
            for j in range(6):
                place = m[:, j:j + 1] * float(slots) + m[:, 6 + j:7 + j]
                same = place == want
                hit = jnp.where(same, 1.0, hit)
                weight = jnp.where(same, m[:, 12 + j:13 + j], weight)
            dm[d] = hit.T.astype(BF)
            cm[d] = weight.astype(BF)

    def dispatch(k):
        @pl.loop(0, 16)
        def _(d):
            z = jnp.dot(dm[d], xr[k, d], preferred_element_type=F32)
            for e in range(experts):
                zs[e, pl.ds(pl.multiple_of(d * slots, 8), slots), :] = z[e * slots:(e + 1) * slots]

    def out_copy(e):
        return pltpu.make_async_copy(hb.at[lax.rem(e, 2)], h_out.at[e], osem.at[lax.rem(e, 2)])

    def expert_step(k, e):
        s = n_shared + k * experts + e
        slot = wait_w(s)
        matmul(zs[e].astype(BF), slot, e, rows, k == 0)
        start_w(s + RING)

        @pl.when(k == nc - 1)
        def _():
            @pl.when(e >= 2)
            def _():
                out_copy(e - 2).wait()

            for n in range(ff // 256):
                cols = slice(256 * n, 256 * (n + 1))
                hb[lax.rem(e, 2), :, cols] = silu_mul(ag[e, :, cols], au[e, :, cols])
            out_copy(e).start()

    hs_copy = pltpu.make_async_copy(hsb, hs_out, osem.at[2])
    cm_copy = pltpu.make_async_copy(cm, cm_out, osem.at[3])
    per_tick = n_shared // 4

    @pl.loop(0, nc + 4)
    def _(t):
        @pl.when(t < nc)
        def _():
            both(t, second)

        @pl.when((t >= 2) & (t < nc + 2))
        def _():
            both(t - 2, third)

        @pl.when(t + 3 < nc)
        def _():
            first(t + 3)

        @pl.when(t < 4)
        def _():
            @pl.loop(0, per_tick)
            def _(j):
                shared_step(t * per_tick + j)

        @pl.when(t == 4)
        def _():
            hs_copy.start()

        @pl.when(t >= 4)
        def _():
            k = t - 4
            both(k, fourth)
            both(k, arrive)

            @pl.when(k == 0)
            def _():
                masks()
                cm_copy.start()

            dispatch(k)

            @pl.loop(0, experts)
            def _(e):
                expert_step(k, e)

    out_copy(experts - 2).wait()
    out_copy(experts - 1).wait()
    hs_copy.wait()
    cm_copy.wait()
    leave(None)

    @pl.loop(0, nc)
    def _(k):
        leave(k)


def down_kernel(h_in, hs_in, cm_in, wd, sd, y_ref, hv, hsv, cmv, wb, os, sums, mine, p1, rd,
                sa, ra, sb, rb, sc, rc, lsem, wsem, ss, rs):
    me = lax.axis_index("ep")
    links, twin = axes(me)
    nc = rd.shape[0]
    experts, rows, ff = hv.shape
    slots = rows // 16
    tokens = y_ref.shape[0]
    tiles = experts + 2
    n_steps = nc * tiles

    def start_w(s):
        slot = lax.rem(s, RING)
        j, t = lax.div(s, tiles), lax.rem(s, tiles)
        cols = pl.ds(pl.multiple_of(j * DC, DC), DC)

        @pl.when((s < n_steps) & (t < experts))
        def _():
            pltpu.make_async_copy(wd.at[t, :, cols], wb.at[slot], wsem.at[slot]).start()

        @pl.when((s < n_steps) & (t >= experts))
        def _():
            part = pl.ds(pl.multiple_of((t - experts) * ff, ff), ff)
            pltpu.make_async_copy(sd.at[part, cols], wb.at[slot], wsem.at[slot]).start()

    def wait_w(s):
        slot = lax.rem(s, RING)
        pltpu.make_async_copy(wd.at[0, :, pl.ds(0, DC)], wb.at[slot], wsem.at[slot]).wait()
        return slot

    loads = [pltpu.make_async_copy(h_in.at[e], hv.at[e], lsem.at[e]) for e in range(experts)]
    loads += [pltpu.make_async_copy(cm_in, cmv, lsem.at[experts]),
              pltpu.make_async_copy(hs_in, hsv, lsem.at[experts + 1])]
    loads[0].start()
    for s in range(RING):
        start_w(s)
    for c in loads[1:]:
        c.start()
    meet(links, twin)

    def copy(kind, i, k):
        if kind == "P":
            src, dst, to, n = p1.at[lax.rem(k, 3)], rd.at[k], twin, 0
        elif kind == "A":
            part = pl.ds(*PARTS[i])
            src, dst, to, n = sa.at[k, part], ra.at[k, part], links[i], 1 + i
        elif kind == "B":
            src, dst, to, n = sb.at[k, i], rb.at[k, i], links[i], 4 + i
        else:
            src, dst, to, n = sc.at[k, i], rc.at[k, i], links[i], 7 + i
        return pltpu.make_async_remote_copy(
            src_ref=src, dst_ref=dst, send_sem=ss.at[k, n], recv_sem=rs.at[k, n],
            device_id={"ep": to}, device_id_type=MESH)

    for c in loads:
        c.wait()

    def project(k):
        @pl.loop(0, experts)
        def _(e):
            s = k * tiles + e
            slot = wait_w(s)
            os[e] = jnp.dot(hv[e], wb[slot], preferred_element_type=F32)
            start_w(s + RING)

    def partial(d):
        o = [os[e, pl.ds(pl.multiple_of(d * slots, 8), slots), :] for e in range(experts)]
        o.append(jnp.zeros((128 - experts * slots, DC), F32))
        return jnp.dot(cmv[d], jnp.concatenate(o, axis=0).astype(BF), preferred_element_type=F32)

    def combine(k):
        slot = lax.rem(k, 3)

        @pl.when(k >= 3)
        def _():
            copy("P", 0, k - 3).wait_send()

        @pl.loop(0, 8)
        def _(q):
            p1[slot, q] = partial(2 * q + 1).astype(BF)

        copy("P", 0, k).start()

        @pl.loop(1, 8)
        def _(q):
            sums[slot, q - 1] = partial(2 * q)

        mine[k] = partial(0)

    def shared(k):
        s = k * tiles + experts
        for half in range(2):
            slot = wait_w(s + half)
            mine[k] += jnp.dot(hsv[:, half * ff:(half + 1) * ff], wb[slot], preferred_element_type=F32)
            start_w(s + half + RING)

    def stage_a(k):
        slot = lax.rem(k, 3)
        copy("P", 0, k).wait_recv()
        sa[k] = (sums[slot, 6] + rd[k, 7].astype(F32)).astype(BF)
        for i in range(3):
            copy("A", i, k).start()

        @pl.loop(1, 7)
        def _(q):
            sums[slot, q - 1] += rd[k, q].astype(F32)

        mine[k] += rd[k, 0].astype(F32)

    def stage_b(k):
        slot = lax.rem(k, 3)
        for i in range(3):
            copy("A", i, k).wait_recv()
            b, q = (i + 1) % 3, 7 ^ BITS[i]
            for p, (start, size) in enumerate(PARTS):
                part = slice(start, start + size)
                v = sums[slot, q - 1, part]
                if p == i:
                    v = v + ra[k, part].astype(F32)
                sb[k, b, part] = v.astype(BF)
            copy("B", b, k).start()

    def stage_c(k):
        slot = lax.rem(k, 3)
        for i in range(3):
            copy("B", i, k).wait_recv()
            c = (i + 1) % 3
            sc[k, c] = (sums[slot, BITS[c] - 1] + rb[k, i].astype(F32)).astype(BF)
            copy("C", c, k).start()

    def finish(k):
        total = mine[k]
        for i in range(3):
            copy("C", i, k).wait_recv()
            total += rc[k, i].astype(F32)
        y_ref[:, pl.ds(pl.multiple_of(k * DC, DC), DC)] = total.astype(BF)

    @pl.loop(0, nc + 5)
    def _(t):
        @pl.when(t < nc)
        def _():
            project(t)

        @pl.when((t >= 1) & (t < nc + 1))
        def _():
            stage_a(t - 1)

        @pl.when((t >= 2) & (t < nc + 2))
        def _():
            stage_b(t - 2)

        @pl.when((t >= 3) & (t < nc + 3))
        def _():
            stage_c(t - 3)

        @pl.when(t < nc)
        def _():
            combine(t)
            shared(t)

        @pl.when(t >= 5)
        def _():
            finish(t - 5)

    @pl.loop(0, nc)
    def _(k):
        @pl.when(k >= nc - 3)
        def _():
            copy("P", 0, k).wait_send()

        for kind in "ABC":
            for i in range(3):
                copy(kind, i, k).wait_send()


def solution(mesh):
    def local(x, expert, slot, gate, w_gate, w_up, w_down, s_gate, s_up, s_down):
        x, expert, slot, gate = x[0, 0], expert[0, 0], slot[0, 0], gate[0, 0]
        tokens, d = x.shape
        top = expert.shape[1]
        experts, _, ff = w_gate.shape
        slots = 5 * tokens * top // (4 * experts * 16)
        rows, nc = 16 * slots, d // DC
        kept = slot < slots
        meta = jnp.concatenate([
            jnp.where(kept, expert, DROPPED).astype(BF), jnp.where(kept, slot, 0).astype(BF), gate.astype(BF),
            jnp.zeros((tokens, 128 - 3 * top), BF)], axis=1)
        dma = pltpu.SemaphoreType.DMA
        vmem = pl.BlockSpec(memory_space=pltpu.VMEM)
        hbm = pl.BlockSpec(memory_space=pl.ANY)
        h, hs, cm = pl.pallas_call(
            up_kernel,
            name="up",
            out_shape=[jax.ShapeDtypeStruct((experts, rows, ff), BF),
                       jax.ShapeDtypeStruct((tokens, 2 * ff), BF),
                       jax.ShapeDtypeStruct((16, tokens, 128), BF)],
            in_specs=[vmem, vmem, hbm, hbm, hbm, hbm],
            out_specs=[hbm, hbm, hbm],
            scratch_shapes=[
                pltpu.VMEM((nc, 16, tokens, DC), BF), pltpu.VMEM((16, tokens, 128), BF),
                pltpu.VMEM((16, 128, tokens), BF), pltpu.VMEM((16, tokens, 128), BF),
                pltpu.VMEM((experts, rows, DC), F32),
                pltpu.VMEM((experts, rows, ff), F32), pltpu.VMEM((experts, rows, ff), F32),
                pltpu.VMEM((RING, 2, DC, ff), BF), pltpu.VMEM((2, rows, ff), BF),
                pltpu.VMEM((tokens, 2 * ff), BF),
                dma((nc + 1, 17)), dma((nc + 1, 17)), dma((RING, 2)), dma((4,))],
            compiler_params=pltpu.CompilerParams(
                collective_id=0, has_side_effects=True, vmem_limit_bytes=67_043_328),
        )(x, meta, w_gate, w_up, s_gate, s_up)
        y = pl.pallas_call(
            down_kernel,
            name="down",
            out_shape=jax.ShapeDtypeStruct((tokens, d), BF),
            in_specs=[hbm] * 5,
            out_specs=vmem,
            scratch_shapes=[
                pltpu.VMEM((experts, rows, ff), BF), pltpu.VMEM((tokens, 2 * ff), BF),
                pltpu.VMEM((16, tokens, 128), BF), pltpu.VMEM((RING, ff, DC), BF),
                pltpu.VMEM((experts, rows, DC), F32), pltpu.VMEM((3, 7, tokens, DC), F32),
                pltpu.VMEM((nc, tokens, DC), F32), pltpu.VMEM((3, 8, tokens, DC), BF),
                pltpu.VMEM((nc, 8, tokens, DC), BF),
                pltpu.VMEM((nc, tokens, DC), BF), pltpu.VMEM((nc, tokens, DC), BF),
                pltpu.VMEM((nc, 3, tokens, DC), BF), pltpu.VMEM((nc, 3, tokens, DC), BF),
                pltpu.VMEM((nc, 3, tokens, DC), BF), pltpu.VMEM((nc, 3, tokens, DC), BF),
                dma((experts + 2,)), dma((RING,)), dma((nc, 10)), dma((nc, 10))],
            compiler_params=pltpu.CompilerParams(
                collective_id=1, has_side_effects=True, vmem_limit_bytes=67_043_328),
        )(h, hs, cm, w_down, s_down)
        return y[None, None]

    tok = P("dp", "ep", None, None)
    return jax.shard_map(
        local, mesh=mesh,
        in_specs=(tok, tok, tok, tok, P("ep"), P("ep"), P("ep"), P(), P(), P()),
        out_specs=tok, check_vma=False)
```

time: 393 us -> 242 us (0.62)
  Pallas kernels: 0 us -> 236 us
  matrix products: 133 us -> 0 us
  waiting for transfers between devices: 125 us -> 0 us
  blocking collectives: 115 us -> 0 us
  local copies, waits for them, and re-layouts: 15.7 us -> 5 us
    pallas_call x0 -> x2, Pallas kernels: none -> 236 us  [the longest x1 142 us: local(): pl.pallas_call(up_kernel, name='up', out_shape=[jax.ShapeDtypeStruct((exp...]
    dot_general x10 -> x0, matrix products: 133 us -> none  [einsum(): return jnp.einsum(form, a.astype(jnp.float32), b.astype(jnp.float32))]
    another operation x1 -> x0, waiting for transfers between devices: 125 us -> none  [placed(): return lax.with_sharding_constraint(v, NamedSharding(mesh, P(*spec)))]
    another operation x1 -> x0, blocking collectives: 115 us -> none  [placed(): return lax.with_sharding_constraint(v, NamedSharding(mesh, P(*spec)))]
    another operation x1 -> x0, local copies, waits for them, and re-layouts: 8.24 us -> none  [placed(): return lax.with_sharding_constraint(v, NamedSharding(mesh, P(*spec)))]
    convert_element_type x3 -> x0, local copies, waits for them, and re-layouts: 5.04 us -> none  [the longest x1 2.45 us: step(): einsum('abtke,abtkc->abtec', to_expert, to_slot).astype(jnp.bfloat16)]
    unnamed x14 -> x4, local copies, waits for them, and re-layouts: 0.67 us -> 4.92 us
  transfers between devices with their start and end apart: 1 -> 0, of which waited for: 1 -> 0; matrix products, arithmetic and copies ran while one was open for 6% -> 0% of each run, Pallas kernels for 0% -> 0%
where the time goes in v1:
time: 242 us; the launch traced here: 241 us
  Pallas kernels  236 us (98%)
  local copies, waits for them, and re-layouts  5 us (2%)
    pallas_call x1, Pallas kernels, local(): pl.pallas_call(up_kernel, name='up', out_shape=[jax.ShapeDtypeStruct((exp...  142 us
    pallas_call x1, Pallas kernels, local(): pl.pallas_call(down_kernel, name='down', out_shape=jax.ShapeDtypeStruct((...  93.4 us
    unnamed x4, local copies, waits for them, and re-layouts  4.92 us

profile of v1, /device:TPU:0, one launch (start us, length us, event | category | flops | bytes accessed | tf_op | source)
XLA Modules:
  0.0 241.5 jit_solution(10894408189116461591)
XLA Ops:
  0.0 0.1 pad.3.clone
  0.1 0.8 copy.13
  0.9 0.8 copy.12
  1.7 0.8 copy.11
  2.6 0.7 maximum_maximum_fusion.m_ref
  3.3 142.3 %up.1 = (bf16[5,384,1536]{2,1,0:T(8,128)(2,1)}, bf16[256,3072]{1,0:T(8,128)(2,1)}, bf16[16,256,128]{2,1,0:T(8,128)(2,1)}) custom-call(bf16[256,2560]{1,0:T(8,128)(2,1)} %bitcast.11, bf16[256,128]{1,0:T(8,128)(2,1)} %maximum_maximum_fusion.m_ref, bf16[5,2560,1536]{2,1,0:T(8,128)(2,1)} %wg.1, bf16[5,2560,1536]{2,1,0:T(8,128)(2,1)} %wu.1, ...), custom_call_target="tpu_custom_call" | custom-call | tf_op jit(solution)/shard_map/up/pallas_call | solution.py:458
  145.6 93.4 %down.1 = bf16[256,2560]{1,0:T(8,128)(2,1)} custom-call(bf16[5,384,1536]{2,1,0:T(8,128)(2,1)} %get-tuple-element.8.h_in, bf16[256,3072]{1,0:T(8,128)(2,1)} %get-tuple-element.9.hs_in, bf16[16,256,128]{2,1,0:T(8,128)(2,1)} %get-tuple-element.10.cm_in, bf16[5,1536,2560]{2,1,0:T(8,128)(2,1)} %wd.1, bf16[3072,2560]{1,0:T(8,128)(2,1)} %sd.1), custom_call_target="tpu_custom_call" | custom-call | tf_op jit(solution)/shard_map/down/pallas_call | solution.py:477
  239.0 2.5 %copy.15 = bf16[1,1,256,2560]{3,2,1,0:T(8,128)(2,1)} copy(bf16[1,1,256,2560]{3,2,1,0:T(8,128)(2,1)} %bitcast.10) | data formatting | bytes 2621440
  (2 shorter events, 0.0 us)

commit v2 on v1

--- a/solution.py
+++ b/solution.py
@@ -13,7 +13,9 @@
 DC = 256
 BITS = (4, 2, 1)
 PARTS = ((0, 96), (96, 80), (176, 80))
-RING = 4
+RING = 3
+RING2 = 8
+KC = 2 * DC
 DROPPED = 128
 
 
@@ -43,16 +45,17 @@
     experts, rows, ff = ag.shape
     tokens = x_ref.shape[0]
     slots = rows // 16
-    n_shared = 2 * nc
-    n_steps = n_shared + nc * experts
+    np_ = nc // 2
+    n_shared = 2 * np_
+    n_steps = n_shared + np_ * experts
 
     def start_w(s):
         slot = lax.rem(s, RING)
 
         @pl.when(s < n_shared)
         def _():
-            half, k = lax.div(s, nc), lax.rem(s, nc)
-            at = (pl.ds(pl.multiple_of(k * DC, DC), DC), pl.ds(pl.multiple_of(half * ff, ff), ff))
+            half, k = lax.div(s, np_), lax.rem(s, np_)
+            at = (pl.ds(pl.multiple_of(k * KC, KC), KC), pl.ds(pl.multiple_of(half * ff, ff), ff))
             for i, w in enumerate((sg, su)):
                 pltpu.make_async_copy(w.at[at], wb.at[slot, i], wsem.at[slot, i]).start()
 
@@ -60,13 +63,13 @@
         def _():
             k, e = lax.div(s - n_shared, experts), lax.rem(s - n_shared, experts)
             for i, w in enumerate((wg, wu)):
-                src = w.at[e, pl.ds(pl.multiple_of(k * DC, DC), DC), :]
+                src = w.at[e, pl.ds(pl.multiple_of(k * KC, KC), KC), :]
                 pltpu.make_async_copy(src, wb.at[slot, i], wsem.at[slot, i]).start()
 
     def wait_w(s):
         slot = lax.rem(s, RING)
         for i, w in enumerate((wg, wu)):
-            pltpu.make_async_copy(w.at[0, pl.ds(0, DC), :], wb.at[slot, i], wsem.at[slot, i]).wait()
+            pltpu.make_async_copy(w.at[0, pl.ds(0, KC), :], wb.at[slot, i], wsem.at[slot, i]).wait()
         return slot
 
     for s in range(RING):
@@ -86,22 +89,16 @@
             src, dst = block(2 * BITS[(i + 1) % 3]), block(2 * (BITS[i] | BITS[(i + 1) % 3]))
             to, n = links[i], 3 + i
         elif kind == "G":
-            part = pl.ds(*PARTS[i])
-            src = block(2 * (BITS[(i + 1) % 3] | BITS[(i + 2) % 3])).at[part]
-            dst, to, n = block(14).at[part], links[i], 6 + i
+            src, dst = block(2 * (BITS[(i + 1) % 3] | BITS[(i + 2) % 3])), block(14)
+            if k is not None:
+                src, dst = src.at[pl.ds(*PARTS[i])], dst.at[pl.ds(*PARTS[i])]
+            to, n = links[i], 6 + i
         else:
             src, dst, to, n = own if i == 0 else block(2 * i), block(2 * i + 1), twin, 9 + i
         return pltpu.make_async_remote_copy(
             src_ref=src, dst_ref=dst, send_sem=ss.at[row, n], recv_sem=rs.at[row, n],
             device_id={"ep": to}, device_id_type=MESH)
 
-    def both(k, do):
-        @pl.when(k == 0)
-        def _():
-            do(None)
-
-        do(k)
-
     def first(k):
         for i in range(3):
             copy("D", i, k).start()
@@ -112,15 +109,20 @@
             copy("F", (i + 2) % 3, k).start()
             copy("S", BITS[i], k).start()
 
+    def whole(k, i):
+        return k is not None or i == 0
+
     def third(k):
         for i in range(3):
             copy("F", i, k).wait_recv()
-            copy("G", (i + 2) % 3, k).start()
+            if whole(k, (i + 2) % 3):
+                copy("G", (i + 2) % 3, k).start()
             copy("S", BITS[i] | BITS[(i + 1) % 3], k).start()
 
     def fourth(k):
         for i in range(3):
-            copy("G", i, k).wait_recv()
+            if whole(k, i):
+                copy("G", i, k).wait_recv()
         copy("S", 7, k).start()
 
     def arrive(k):
@@ -130,10 +132,11 @@
     def leave(k):
         for kind, count in (("D", 3), ("F", 3), ("G", 3), ("S", 8)):
             for i in range(count):
-                copy(kind, i, k).wait_send()
+                if kind != "G" or whole(k, i):
+                    copy(kind, i, k).wait_send()
 
     first(None)
-    for k in range(3):
+    for k in range(2):
         first(k)
     copy("S", 0, None).start()
 
@@ -144,115 +147,153 @@
 
     mr[0] = m_ref[...]
 
-    def matmul(lhs, slot, e, m, fresh):
-        for n in range(ff // 256):
-            cols = slice(256 * n, 256 * (n + 1))
-            for i, acc in enumerate((ag, au)):
-                old = jnp.where(fresh, 0.0, acc[e, :m, cols])
-                acc[e, :m, cols] = old + jnp.dot(lhs, wb[slot, i, :, cols], preferred_element_type=F32)
+    def matmul(lhs, slot, e, k, emit):
+        m = lhs.shape[0]
+
+        def dots(cols):
+            return [jnp.dot(lhs, wb[slot, i, :, cols], preferred_element_type=F32) for i in range(2)]
+
+        tiles = [(n, slice(256 * n, 256 * (n + 1))) for n in range(ff // 256)]
+
+        @pl.when(k == 0)
+        def _():
+            for n, cols in tiles:
+                ag[e, :m, cols], au[e, :m, cols] = dots(cols)
+
+        @pl.when((k > 0) & (k < np_ - 1))
+        def _():
+            for n, cols in tiles:
+                g, u = dots(cols)
+                ag[e, :m, cols] += g
+                au[e, :m, cols] += u
+
+        @pl.when(k == np_ - 1)
+        def _():
+            for n, cols in tiles:
+                g, u = dots(cols)
+                emit(n, silu_mul(ag[e, :m, cols] + g, au[e, :m, cols] + u))
 
     def shared_step(s):
         slot = wait_w(s)
-        half, k = lax.div(s, nc), lax.rem(s, nc)
-        matmul(xr[k, 0], slot, 0, tokens, k == 0)
+        half, k = lax.div(s, np_), lax.rem(s, np_)
+
+        def emit(n, v):
+            hsb[:, pl.ds(pl.multiple_of(half * ff + 256 * n, 256), 256)] = v
+
+        matmul(x_ref[:, pl.ds(pl.multiple_of(k * KC, KC), KC)], slot, 0, k, emit)
         start_w(s + RING)
-
-        @pl.when(k == nc - 1)
-        def _():
-            for n in range(ff // 256):
-                cols = slice(256 * n, 256 * (n + 1))
-                at = pl.ds(pl.multiple_of(half * ff + 256 * n, 256), 256)
-                hsb[:, at] = silu_mul(ag[0, :tokens, cols], au[0, :tokens, cols])
 
     def masks():
         base = (me * (experts * slots)).astype(F32)
-        lane = lax.broadcasted_iota(jnp.int32, (tokens, 128), 1)
-        want = jnp.where(lane < experts * slots, lane.astype(F32) + base, -1.0)
+        row = lax.broadcasted_iota(jnp.int32, (128, tokens), 0)
+        want = jnp.where(row < experts * slots, row.astype(F32) + base, -1.0)
 
         @pl.loop(0, 16)
         def _(d):
             m = mr[d].astype(F32)
-            hit = jnp.zeros((tokens, 128), F32)
-            weight = jnp.zeros((tokens, 128), F32)
+            hit = jnp.zeros((128, tokens), F32)
+            weight = jnp.zeros((128, tokens), F32)
             for j in range(6):
-                place = m[:, j:j + 1] * float(slots) + m[:, 6 + j:7 + j]
+                place = m[j:j + 1] * float(slots) + m[6 + j:7 + j]
                 same = place == want
                 hit = jnp.where(same, 1.0, hit)
-                weight = jnp.where(same, m[:, 12 + j:13 + j], weight)
-            dm[d] = hit.T.astype(BF)
-            cm[d] = weight.astype(BF)
-
-    def dispatch(k):
-        @pl.loop(0, 16)
-        def _(d):
-            z = jnp.dot(dm[d], xr[k, d], preferred_element_type=F32)
-            for e in range(experts):
-                zs[e, pl.ds(pl.multiple_of(d * slots, 8), slots), :] = z[e * slots:(e + 1) * slots]
+                weight = jnp.where(same, m[12 + j:13 + j], weight)
+            dm[d] = hit.astype(BF)
+            cm[d] = weight.T.astype(BF)
+
+    def dispatch(p):
+        for half in range(2):
+            cols = slice(half * DC, (half + 1) * DC)
+            for q in range(8):
+                z = [jnp.dot(dm[2 * q + c], xr[2 * p + half, 2 * q + c], preferred_element_type=F32) for c in range(2)]
+                for e in range(experts):
+                    pair = [v[e * slots:(e + 1) * slots] for v in z]
+                    zs[e, 2 * q * slots:2 * (q + 1) * slots, cols] = jnp.concatenate(pair, axis=0).astype(BF)
 
     def out_copy(e):
         return pltpu.make_async_copy(hb.at[lax.rem(e, 2)], h_out.at[e], osem.at[lax.rem(e, 2)])
 
-    def expert_step(k, e):
-        s = n_shared + k * experts + e
+    def expert_step(p, e):
+        s = n_shared + p * experts + e
         slot = wait_w(s)
-        matmul(zs[e].astype(BF), slot, e, rows, k == 0)
+
+        @pl.when((p == np_ - 1) & (e >= 2))
+        def _():
+            out_copy(e - 2).wait()
+
+        def emit(n, v):
+            hb[lax.rem(e, 2), :, 256 * n:256 * (n + 1)] = v
+
+        matmul(zs[e], slot, e, p, emit)
         start_w(s + RING)
 
-        @pl.when(k == nc - 1)
-        def _():
-            @pl.when(e >= 2)
-            def _():
-                out_copy(e - 2).wait()
-
-            for n in range(ff // 256):
-                cols = slice(256 * n, 256 * (n + 1))
-                hb[lax.rem(e, 2), :, cols] = silu_mul(ag[e, :, cols], au[e, :, cols])
+        @pl.when(p == np_ - 1)
+        def _():
             out_copy(e).start()
 
     hs_copy = pltpu.make_async_copy(hsb, hs_out, osem.at[2])
     cm_copy = pltpu.make_async_copy(cm, cm_out, osem.at[3])
-    per_tick = n_shared // 4
+    split = 2
 
     @pl.loop(0, nc + 4)
     def _(t):
+        for step, do in enumerate((second, third, fourth)):
+            @pl.when(t == step)
+            def _():
+                do(None)
+
         @pl.when(t < nc)
         def _():
-            both(t, second)
+            second(t)
+
+        @pl.when((t >= 1) & (t < nc + 1))
+        def _():
+            third(t - 1)
+
+        @pl.when(t + 2 < nc)
+        def _():
+            first(t + 2)
 
         @pl.when((t >= 2) & (t < nc + 2))
         def _():
-            both(t - 2, third)
-
-        @pl.when(t + 3 < nc)
-        def _():
-            first(t + 3)
-
-        @pl.when(t < 4)
-        def _():
-            @pl.loop(0, per_tick)
+            fourth(t - 2)
+
+        @pl.when(t == 3)
+        def _():
+            hs_copy.start()
+            cm_copy.start()
+
+        @pl.when(t < 3)
+        def _():
+            @pl.loop(0, 4)
             def _(j):
-                shared_step(t * per_tick + j)
-
-        @pl.when(t == 4)
-        def _():
-            hs_copy.start()
-
-        @pl.when(t >= 4)
-        def _():
-            k = t - 4
-            both(k, fourth)
-            both(k, arrive)
-
-            @pl.when(k == 0)
-            def _():
-                masks()
-                cm_copy.start()
-
-            dispatch(k)
-
-            @pl.loop(0, experts)
+                @pl.when(4 * t + j < n_shared)
+                def _():
+                    shared_step(4 * t + j)
+
+        @pl.when(t == 2)
+        def _():
+            arrive(None)
+            masks()
+
+        p = lax.div(t - 3, 2)
+        early = lax.rem(t, 2) == 1
+
+        @pl.when((t >= 3) & (t < nc + 3) & early)
+        def _():
+            arrive(2 * p)
+            arrive(2 * p + 1)
+            dispatch(p)
+
+            @pl.loop(0, split)
             def _(e):
-                expert_step(k, e)
+                expert_step(p, e)
+
+        @pl.when((t >= 4) & (t < nc + 4) & ~early)
+        def _():
+            @pl.loop(split, experts)
+            def _(e):
+                expert_step(p, e)
 
     out_copy(experts - 2).wait()
     out_copy(experts - 1).wait()
@@ -277,7 +318,7 @@
     n_steps = nc * tiles
 
     def start_w(s):
-        slot = lax.rem(s, RING)
+        slot = lax.rem(s, RING2)
         j, t = lax.div(s, tiles), lax.rem(s, tiles)
         cols = pl.ds(pl.multiple_of(j * DC, DC), DC)
 
@@ -291,7 +332,7 @@
             pltpu.make_async_copy(sd.at[part, cols], wb.at[slot], wsem.at[slot]).start()
 
     def wait_w(s):
-        slot = lax.rem(s, RING)
+        slot = lax.rem(s, RING2)
         pltpu.make_async_copy(wd.at[0, :, pl.ds(0, DC)], wb.at[slot], wsem.at[slot]).wait()
         return slot
 
@@ -299,7 +340,7 @@
     loads += [pltpu.make_async_copy(cm_in, cmv, lsem.at[experts]),
               pltpu.make_async_copy(hs_in, hsv, lsem.at[experts + 1])]
     loads[0].start()
-    for s in range(RING):
+    for s in range(RING2):
         start_w(s)
     for c in loads[1:]:
         c.start()
@@ -323,15 +364,14 @@
         c.wait()
 
     def project(k):
-        @pl.loop(0, experts)
-        def _(e):
-            s = k * tiles + e
-            slot = wait_w(s)
+        held = [wait_w(k * tiles + e) for e in range(experts)]
+        for e, slot in enumerate(held):
             os[e] = jnp.dot(hv[e], wb[slot], preferred_element_type=F32)
-            start_w(s + RING)
+        for e in range(experts):
+            start_w(k * tiles + e + RING2)
 
     def partial(d):
-        o = [os[e, pl.ds(pl.multiple_of(d * slots, 8), slots), :] for e in range(experts)]
+        o = [os[e, d * slots:(d + 1) * slots, :] for e in range(experts)]
         o.append(jnp.zeros((128 - experts * slots, DC), F32))
         return jnp.dot(cmv[d], jnp.concatenate(o, axis=0).astype(BF), preferred_element_type=F32)
 
@@ -342,24 +382,22 @@
         def _():
             copy("P", 0, k - 3).wait_send()
 
-        @pl.loop(0, 8)
-        def _(q):
+        for q in range(8):
             p1[slot, q] = partial(2 * q + 1).astype(BF)
 
         copy("P", 0, k).start()
 
-        @pl.loop(1, 8)
-        def _(q):
+        for q in range(1, 8):
             sums[slot, q - 1] = partial(2 * q)
 
         mine[k] = partial(0)
 
     def shared(k):
-        s = k * tiles + experts
+        held = [wait_w(k * tiles + experts + half) for half in range(2)]
+        mine[k] += sum(jnp.dot(hsv[:, half * ff:(half + 1) * ff], wb[slot], preferred_element_type=F32)
+                       for half, slot in enumerate(held))
         for half in range(2):
-            slot = wait_w(s + half)
-            mine[k] += jnp.dot(hsv[:, half * ff:(half + 1) * ff], wb[slot], preferred_element_type=F32)
-            start_w(s + half + RING)
+            start_w(k * tiles + experts + half + RING2)
 
     def stage_a(k):
         slot = lax.rem(k, 3)
@@ -402,23 +440,25 @@
             total += rc[k, i].astype(F32)
         y_ref[:, pl.ds(pl.multiple_of(k * DC, DC), DC)] = total.astype(BF)
 
+    quick = 2
+
     @pl.loop(0, nc + 5)
     def _(t):
         @pl.when(t < nc)
         def _():
             project(t)
 
-        @pl.when((t >= 1) & (t < nc + 1))
-        def _():
-            stage_a(t - 1)
-
-        @pl.when((t >= 2) & (t < nc + 2))
-        def _():
-            stage_b(t - 2)
-
-        @pl.when((t >= 3) & (t < nc + 3))
-        def _():
-            stage_c(t - 3)
+        kb = jnp.where(t <= quick, t - 1, t - 2)
+
+        @pl.when((t >= 1) & (t != quick + 1) & (t < nc + 2))
+        def _():
+            stage_b(kb)
+
+        kc = jnp.where(t <= quick + 1, t - 2, t - 3)
+
+        @pl.when((t >= 2) & (t != quick + 2) & (t < nc + 3))
+        def _():
+            stage_c(kc)
 
         @pl.when(t < nc)
         def _():
@@ -428,6 +468,10 @@
         @pl.when(t >= 5)
         def _():
             finish(t - 5)
+
+        @pl.when(t < nc)
+        def _():
+            stage_a(t)
 
     @pl.loop(0, nc)
     def _(k):
@@ -450,8 +494,8 @@
         rows, nc = 16 * slots, d // DC
         kept = slot < slots
         meta = jnp.concatenate([
-            jnp.where(kept, expert, DROPPED).astype(BF), jnp.where(kept, slot, 0).astype(BF), gate.astype(BF),
-            jnp.zeros((tokens, 128 - 3 * top), BF)], axis=1)
+            jnp.where(kept, expert, DROPPED).astype(BF).T, jnp.where(kept, slot, 0).astype(BF).T,
+            gate.astype(BF).T, jnp.zeros((32 - 3 * top, tokens), BF)], axis=0)
         dma = pltpu.SemaphoreType.DMA
         vmem = pl.BlockSpec(memory_space=pltpu.VMEM)
         hbm = pl.BlockSpec(memory_space=pl.ANY)
@@ -464,11 +508,11 @@
             in_specs=[vmem, vmem, hbm, hbm, hbm, hbm],
             out_specs=[hbm, hbm, hbm],
             scratch_shapes=[
-                pltpu.VMEM((nc, 16, tokens, DC), BF), pltpu.VMEM((16, tokens, 128), BF),
+                pltpu.VMEM((nc, 16, tokens, DC), BF), pltpu.VMEM((16, 32, tokens), BF),
                 pltpu.VMEM((16, 128, tokens), BF), pltpu.VMEM((16, tokens, 128), BF),
-                pltpu.VMEM((experts, rows, DC), F32),
+                pltpu.VMEM((experts, rows, KC), BF),
                 pltpu.VMEM((experts, rows, ff), F32), pltpu.VMEM((experts, rows, ff), F32),
-                pltpu.VMEM((RING, 2, DC, ff), BF), pltpu.VMEM((2, rows, ff), BF),
+                pltpu.VMEM((RING, 2, KC, ff), BF), pltpu.VMEM((2, rows, ff), BF),
                 pltpu.VMEM((tokens, 2 * ff), BF),
                 dma((nc + 1, 17)), dma((nc + 1, 17)), dma((RING, 2)), dma((4,))],
             compiler_params=pltpu.CompilerParams(
@@ -482,14 +526,14 @@
             out_specs=vmem,
             scratch_shapes=[
                 pltpu.VMEM((experts, rows, ff), BF), pltpu.VMEM((tokens, 2 * ff), BF),
-                pltpu.VMEM((16, tokens, 128), BF), pltpu.VMEM((RING, ff, DC), BF),
+                pltpu.VMEM((16, tokens, 128), BF), pltpu.VMEM((RING2, ff, DC), BF),
                 pltpu.VMEM((experts, rows, DC), F32), pltpu.VMEM((3, 7, tokens, DC), F32),
                 pltpu.VMEM((nc, tokens, DC), F32), pltpu.VMEM((3, 8, tokens, DC), BF),
                 pltpu.VMEM((nc, 8, tokens, DC), BF),
                 pltpu.VMEM((nc, tokens, DC), BF), pltpu.VMEM((nc, tokens, DC), BF),
                 pltpu.VMEM((nc, 3, tokens, DC), BF), pltpu.VMEM((nc, 3, tokens, DC), BF),
                 pltpu.VMEM((nc, 3, tokens, DC), BF), pltpu.VMEM((nc, 3, tokens, DC), BF),
-                dma((experts + 2,)), dma((RING,)), dma((nc, 10)), dma((nc, 10))],
+                dma((experts + 2,)), dma((RING2,)), dma((nc, 10)), dma((nc, 10))],
             compiler_params=pltpu.CompilerParams(
                 collective_id=1, has_side_effects=True, vmem_limit_bytes=67_043_328),
         )(h, hs, cm, w_down, s_down)

time: 242 us -> 187 us (0.77)
  Pallas kernels: 236 us -> 182 us
    pallas_call x1, Pallas kernels: 142 us -> 94.3 us  [local(): pl.pallas_call(up_kernel, name='up', out_shape=[jax.ShapeDtypeStruct((exp...]
    pallas_call x1, Pallas kernels: 93.4 us -> 87.6 us  [local(): pl.pallas_call(down_kernel, name='down', out_shape=jax.ShapeDtypeStruct((...]
    unnamed x4 -> x2, local copies, waits for them, and re-layouts: 4.92 us -> 3.15 us
where the time goes in v2:
time: 187 us
  Pallas kernels  182 us (97%)
  local copies, waits for them, and re-layouts  3.23 us (2%)
    pallas_call x1, Pallas kernels, local(): pl.pallas_call(up_kernel, name='up', out_shape=[jax.ShapeDtypeStruct((exp...  94.3 us
    pallas_call x1, Pallas kernels, local(): pl.pallas_call(down_kernel, name='down', out_shape=jax.ShapeDtypeStruct((...  87.6 us

profile of v2, /device:TPU:0, one launch (start us, length us, event | category | flops | bytes accessed | tf_op | source)
XLA Modules:
  0.0 186.5 jit_solution(4943285243992976306)
XLA Ops:
  0.0 0.1 pad.3.clone
  0.1 0.7 copy.26
  0.8 0.7 fusion.4
  1.5 0.7 maximum_maximum_fusion.m_ref
  2.2 94.3 %up.1 = (bf16[5,384,1536]{2,1,0:T(8,128)(2,1)}, bf16[256,3072]{1,0:T(8,128)(2,1)}, bf16[16,256,128]{2,1,0:T(8,128)(2,1)}) custom-call(bf16[256,2560]{1,0:T(8,128)(2,1)} %bitcast.23, bf16[32,256]{1,0:T(8,128)(2,1)} %maximum_maximum_fusion.m_ref, bf16[5,2560,1536]{2,1,0:T(8,128)(2,1)} %wg.1, bf16[5,2560,1536]{2,1,0:T(8,128)(2,1)} %wu.1, ...), custom_call_target="tpu_custom_call" | custom-call | tf_op jit(solution)/shard_map/up/pallas_call | solution.py:502
  96.5 87.6 %down.1 = bf16[256,2560]{1,0:T(8,128)(2,1)} custom-call(bf16[5,384,1536]{2,1,0:T(8,128)(2,1)} %get-tuple-element.8.h_in, bf16[256,3072]{1,0:T(8,128)(2,1)} %get-tuple-element.9.hs_in, bf16[16,256,128]{2,1,0:T(8,128)(2,1)} %get-tuple-element.10.cm_in, bf16[5,1536,2560]{2,1,0:T(8,128)(2,1)} %wd.1, bf16[3072,2560]{1,0:T(8,128)(2,1)} %sd.1), custom_call_target="tpu_custom_call" | custom-call | tf_op jit(solution)/shard_map/down/pallas_call | solution.py:521
  184.1 2.5 %copy.28 = bf16[1,1,256,2560]{3,2,1,0:T(8,128)(2,1)} copy(bf16[1,1,256,2560]{3,2,1,0:T(8,128)(2,1)} %bitcast.22) | data formatting | bytes 2621440
  (1 shorter events, 0.0 us)

commit v3 on v2

--- a/solution.py
+++ b/solution.py
@@ -13,6 +13,9 @@
 DC = 256
 BITS = (4, 2, 1)
 PARTS = ((0, 96), (96, 80), (176, 80))
+REST = (((96, 160),), ((0, 96), (176, 80)), ((0, 176),))
+ORDER = (7, 6, 5, 3, 1, 2, 4, 0)
+EARLY = tuple((b, rest) for b in range(3) for rest in REST[(b + 2) % 3])
 RING = 3
 RING2 = 8
 KC = 2 * DC
@@ -76,7 +79,7 @@
         start_w(s)
     meet(links, twin)
 
-    def copy(kind, i, k):
+    def copy(kind, i, k, turn=0):
         row = nc if k is None else k
         own = m_ref if k is None else x_ref.at[:, pl.ds(pl.multiple_of(k * DC, DC), DC)]
 
@@ -91,7 +94,8 @@
         elif kind == "G":
             src, dst = block(2 * (BITS[(i + 1) % 3] | BITS[(i + 2) % 3])), block(14)
             if k is not None:
-                src, dst = src.at[pl.ds(*PARTS[i])], dst.at[pl.ds(*PARTS[i])]
+                part = pl.ds(*PARTS[(i + turn) % 3])
+                src, dst = src.at[part], dst.at[part]
             to, n = links[i], 6 + i
         else:
             src, dst, to, n = own if i == 0 else block(2 * i), block(2 * i + 1), twin, 9 + i
@@ -109,20 +113,25 @@
             copy("F", (i + 2) % 3, k).start()
             copy("S", BITS[i], k).start()
 
-    def whole(k, i):
-        return k is not None or i == 0
+    def each(k, do):
+        if k is None:
+            do(copy("G", 0, None))
+            return
+        for turn in range(3):
+            @pl.when(lax.rem(k, 3) == turn)
+            def _():
+                for i in range(3):
+                    do(copy("G", i, k, turn))
 
     def third(k):
         for i in range(3):
             copy("F", i, k).wait_recv()
-            if whole(k, (i + 2) % 3):
-                copy("G", (i + 2) % 3, k).start()
+        each(k, lambda c: c.start())
+        for i in range(3):
             copy("S", BITS[i] | BITS[(i + 1) % 3], k).start()
 
     def fourth(k):
-        for i in range(3):
-            if whole(k, i):
-                copy("G", i, k).wait_recv()
+        each(k, lambda c: c.wait_recv())
         copy("S", 7, k).start()
 
     def arrive(k):
@@ -130,10 +139,10 @@
             copy("S", q, k).wait_recv()
 
     def leave(k):
-        for kind, count in (("D", 3), ("F", 3), ("G", 3), ("S", 8)):
+        for kind, count in (("D", 3), ("F", 3), ("S", 8)):
             for i in range(count):
-                if kind != "G" or whole(k, i):
-                    copy(kind, i, k).wait_send()
+                copy(kind, i, k).wait_send()
+        each(k, lambda c: c.wait_send())
 
     first(None)
     for k in range(2):
@@ -339,28 +348,33 @@
     loads = [pltpu.make_async_copy(h_in.at[e], hv.at[e], lsem.at[e]) for e in range(experts)]
     loads += [pltpu.make_async_copy(cm_in, cmv, lsem.at[experts]),
               pltpu.make_async_copy(hs_in, hsv, lsem.at[experts + 1])]
-    loads[0].start()
     for s in range(RING2):
         start_w(s)
-    for c in loads[1:]:
-        c.start()
+        if s < experts + 1:
+            loads[s].start()
+    loads[experts + 1].start()
     meet(links, twin)
 
     def copy(kind, i, k):
         if kind == "P":
-            src, dst, to, n = p1.at[lax.rem(k, 3)], rd.at[k], twin, 0
+            part = pl.ds(4 * i, 4)
+            src, dst, to, n = p1.at[lax.rem(k, 3), part], rd.at[k, part], twin, 14 * i
         elif kind == "A":
             part = pl.ds(*PARTS[i])
             src, dst, to, n = sa.at[k, part], ra.at[k, part], links[i], 1 + i
         elif kind == "B":
-            src, dst, to, n = sb.at[k, i], rb.at[k, i], links[i], 4 + i
+            part = pl.ds(*PARTS[(i + 2) % 3])
+            src, dst, to, n = sb.at[k, i, part], rb.at[k, i, part], links[i], 4 + i
+        elif kind == "E":
+            b, rest = EARLY[i]
+            src, dst, to, n = sb.at[k, b, pl.ds(*rest)], rb.at[k, b, pl.ds(*rest)], links[b], 10 + i
         else:
             src, dst, to, n = sc.at[k, i], rc.at[k, i], links[i], 7 + i
         return pltpu.make_async_remote_copy(
             src_ref=src, dst_ref=dst, send_sem=ss.at[k, n], recv_sem=rs.at[k, n],
             device_id={"ep": to}, device_id_type=MESH)
 
-    for c in loads:
+    for c in loads[:experts]:
         c.wait()
 
     def project(k):
@@ -380,12 +394,13 @@
 
         @pl.when(k >= 3)
         def _():
-            copy("P", 0, k - 3).wait_send()
-
-        for q in range(8):
-            p1[slot, q] = partial(2 * q + 1).astype(BF)
-
-        copy("P", 0, k).start()
+            for half in range(2):
+                copy("P", half, k - 3).wait_send()
+
+        for half in range(2):
+            for n in range(4 * half, 4 * half + 4):
+                p1[slot, n] = partial(2 * ORDER[n] + 1).astype(BF)
+            copy("P", half, k).start()
 
         for q in range(1, 8):
             sums[slot, q - 1] = partial(2 * q)
@@ -401,33 +416,42 @@
 
     def stage_a(k):
         slot = lax.rem(k, 3)
+
+        def other(q):
+            return rd[k, ORDER.index(q)].astype(F32)
+
         copy("P", 0, k).wait_recv()
-        sa[k] = (sums[slot, 6] + rd[k, 7].astype(F32)).astype(BF)
+        sa[k] = (sums[slot, 6] + other(7)).astype(BF)
         for i in range(3):
             copy("A", i, k).start()
-
-        @pl.loop(1, 7)
-        def _(q):
-            sums[slot, q - 1] += rd[k, q].astype(F32)
-
-        mine[k] += rd[k, 0].astype(F32)
+        for b in range(3):
+            q = 7 ^ BITS[(b + 2) % 3]
+            sums[slot, q - 1] += other(q)
+            for n, (owner, (start, size)) in enumerate(EARLY):
+                if owner == b:
+                    rest = slice(start, start + size)
+                    sb[k, b, rest] = sums[slot, q - 1, rest].astype(BF)
+                    copy("E", n, k).start()
+        copy("P", 1, k).wait_recv()
+        for q in (1, 2, 4):
+            sums[slot, q - 1] += other(q)
+        mine[k] += other(0)
 
     def stage_b(k):
         slot = lax.rem(k, 3)
         for i in range(3):
             copy("A", i, k).wait_recv()
             b, q = (i + 1) % 3, 7 ^ BITS[i]
-            for p, (start, size) in enumerate(PARTS):
-                part = slice(start, start + size)
-                v = sums[slot, q - 1, part]
-                if p == i:
-                    v = v + ra[k, part].astype(F32)
-                sb[k, b, part] = v.astype(BF)
+            part = slice(PARTS[i][0], PARTS[i][0] + PARTS[i][1])
+            sb[k, b, part] = (sums[slot, q - 1, part] + ra[k, part].astype(F32)).astype(BF)
             copy("B", b, k).start()
 
     def stage_c(k):
         slot = lax.rem(k, 3)
         for i in range(3):
+            for n, (owner, rest) in enumerate(EARLY):
+                if owner == i:
+                    copy("E", n, k).wait_recv()
             copy("B", i, k).wait_recv()
             c = (i + 1) % 3
             sc[k, c] = (sums[slot, BITS[c] - 1] + rb[k, i].astype(F32)).astype(BF)
@@ -460,16 +484,28 @@
         def _():
             stage_c(kc)
 
+        @pl.when(t == 0)
+        def _():
+            loads[experts].wait()
+
         @pl.when(t < nc)
         def _():
             combine(t)
+
+        @pl.when(t == 0)
+        def _():
+            stage_a(t)
+            loads[experts + 1].wait()
+
+        @pl.when(t < nc)
+        def _():
             shared(t)
 
         @pl.when(t >= 5)
         def _():
             finish(t - 5)
 
-        @pl.when(t < nc)
+        @pl.when((t > 0) & (t < nc))
         def _():
             stage_a(t)
 
@@ -477,10 +513,11 @@
     def _(k):
         @pl.when(k >= nc - 3)
         def _():
-            copy("P", 0, k).wait_send()
-
-        for kind in "ABC":
-            for i in range(3):
+            for half in range(2):
+                copy("P", half, k).wait_send()
+
+        for kind, count in (("A", 3), ("B", 3), ("C", 3), ("E", len(EARLY))):
+            for i in range(count):
                 copy(kind, i, k).wait_send()
 
 
@@ -533,7 +570,7 @@
                 pltpu.VMEM((nc, tokens, DC), BF), pltpu.VMEM((nc, tokens, DC), BF),
                 pltpu.VMEM((nc, 3, tokens, DC), BF), pltpu.VMEM((nc, 3, tokens, DC), BF),
                 pltpu.VMEM((nc, 3, tokens, DC), BF), pltpu.VMEM((nc, 3, tokens, DC), BF),
-                dma((experts + 2,)), dma((RING2,)), dma((nc, 10)), dma((nc, 10))],
+                dma((experts + 2,)), dma((RING2,)), dma((nc, 15)), dma((nc, 15))],
             compiler_params=pltpu.CompilerParams(
                 collective_id=1, has_side_effects=True, vmem_limit_bytes=67_043_328),
         )(h, hs, cm, w_down, s_down)

time: 187 us -> 180 us (0.963)
  Pallas kernels: 182 us -> 175 us
    pallas_call x1, Pallas kernels: 87.6 us -> 82.4 us  [local(): pl.pallas_call(down_kernel, name='down', out_shape=jax.ShapeDtypeStruct((...]
where the time goes in v3:
time: 180 us
  Pallas kernels  175 us (97%)
  local copies, waits for them, and re-layouts  3.23 us (2%)
    pallas_call x1, Pallas kernels, local(): pl.pallas_call(up_kernel, name='up', out_shape=[jax.ShapeDtypeStruct((exp...  92.7 us
    pallas_call x1, Pallas kernels, local(): pl.pallas_call(down_kernel, name='down', out_shape=jax.ShapeDtypeStruct((...  82.4 us

profile of v3, /device:TPU:0, one launch (start us, length us, event | category | flops | bytes accessed | tf_op | source)
XLA Modules:
  0.0 179.8 jit_solution(15809679010894914452)
XLA Ops:
  0.0 0.1 pad.3.clone
  0.1 0.7 copy.26
  0.8 0.7 fusion.4
  1.5 0.7 maximum_maximum_fusion.m_ref
  2.2 92.7 %up.1 = (bf16[5,384,1536]{2,1,0:T(8,128)(2,1)}, bf16[256,3072]{1,0:T(8,128)(2,1)}, bf16[16,256,128]{2,1,0:T(8,128)(2,1)}) custom-call(bf16[256,2560]{1,0:T(8,128)(2,1)} %bitcast.23, bf16[32,256]{1,0:T(8,128)(2,1)} %maximum_maximum_fusion.m_ref, bf16[5,2560,1536]{2,1,0:T(8,128)(2,1)} %wg.1, bf16[5,2560,1536]{2,1,0:T(8,128)(2,1)} %wu.1, ...), custom_call_target="tpu_custom_call" | custom-call | tf_op jit(solution)/shard_map/up/pallas_call | solution.py:539
  94.9 82.4 %down.1 = bf16[256,2560]{1,0:T(8,128)(2,1)} custom-call(bf16[5,384,1536]{2,1,0:T(8,128)(2,1)} %get-tuple-element.8.h_in, bf16[256,3072]{1,0:T(8,128)(2,1)} %get-tuple-element.9.hs_in, bf16[16,256,128]{2,1,0:T(8,128)(2,1)} %get-tuple-element.10.cm_in, bf16[5,1536,2560]{2,1,0:T(8,128)(2,1)} %wd.1, bf16[3072,2560]{1,0:T(8,128)(2,1)} %sd.1), custom_call_target="tpu_custom_call" | custom-call | tf_op jit(solution)/shard_map/down/pallas_call | solution.py:558
  177.3 2.5 %copy.28 = bf16[1,1,256,2560]{3,2,1,0:T(8,128)(2,1)} copy(bf16[1,1,256,2560]{3,2,1,0:T(8,128)(2,1)} %bitcast.22) | data formatting | bytes 2621440
  (1 shorter events, 0.0 us)

commit v4 on v3

--- a/solution.py
+++ b/solution.py
@@ -15,7 +15,7 @@
 PARTS = ((0, 96), (96, 80), (176, 80))
 REST = (((96, 160),), ((0, 96), (176, 80)), ((0, 176),))
 ORDER = (7, 6, 5, 3, 1, 2, 4, 0)
-EARLY = tuple((b, rest) for b in range(3) for rest in REST[(b + 2) % 3])
+EARLY = [[(b, rest) for b in range(3) for rest in REST[(b + 2 + turn) % 3]] for turn in range(3)]
 RING = 3
 RING2 = 8
 KC = 2 * DC
@@ -242,7 +242,7 @@
 
     hs_copy = pltpu.make_async_copy(hsb, hs_out, osem.at[2])
     cm_copy = pltpu.make_async_copy(cm, cm_out, osem.at[3])
-    split = 2
+    split = 3
 
     @pl.loop(0, nc + 4)
     def _(t):
@@ -355,18 +355,24 @@
     loads[experts + 1].start()
     meet(links, twin)
 
-    def copy(kind, i, k):
+    def by_turns(k, do):
+        for turn in range(3):
+            @pl.when(lax.rem(k, 3) == turn)
+            def _():
+                do(k, turn)
+
+    def copy(kind, i, k, turn=0):
         if kind == "P":
             part = pl.ds(4 * i, 4)
             src, dst, to, n = p1.at[lax.rem(k, 3), part], rd.at[k, part], twin, 14 * i
         elif kind == "A":
-            part = pl.ds(*PARTS[i])
+            part = pl.ds(*PARTS[(i + turn) % 3])
             src, dst, to, n = sa.at[k, part], ra.at[k, part], links[i], 1 + i
         elif kind == "B":
-            part = pl.ds(*PARTS[(i + 2) % 3])
+            part = pl.ds(*PARTS[(i + 2 + turn) % 3])
             src, dst, to, n = sb.at[k, i, part], rb.at[k, i, part], links[i], 4 + i
         elif kind == "E":
-            b, rest = EARLY[i]
+            b, rest = EARLY[turn][i]
             src, dst, to, n = sb.at[k, b, pl.ds(*rest)], rb.at[k, b, pl.ds(*rest)], links[b], 10 + i
         else:
             src, dst, to, n = sc.at[k, i], rc.at[k, i], links[i], 7 + i
@@ -374,9 +380,6 @@
             src_ref=src, dst_ref=dst, send_sem=ss.at[k, n], recv_sem=rs.at[k, n],
             device_id={"ep": to}, device_id_type=MESH)
 
-    for c in loads[:experts]:
-        c.wait()
-
     def project(k):
         held = [wait_w(k * tiles + e) for e in range(experts)]
         for e, slot in enumerate(held):
@@ -384,6 +387,12 @@
         for e in range(experts):
             start_w(k * tiles + e + RING2)
 
+    for e in range(experts):
+        loads[e].wait()
+        os[e] = jnp.dot(hv[e], wb[wait_w(e)], preferred_element_type=F32)
+        start_w(e + RING2)
+    loads[experts].wait()
+
     def partial(d):
         o = [os[e, d * slots:(d + 1) * slots, :] for e in range(experts)]
         o.append(jnp.zeros((128 - experts * slots, DC), F32))
@@ -414,7 +423,7 @@
         for half in range(2):
             start_w(k * tiles + experts + half + RING2)
 
-    def stage_a(k):
+    def stage_a(k, turn):
         slot = lax.rem(k, 3)
 
         def other(q):
@@ -423,36 +432,37 @@
         copy("P", 0, k).wait_recv()
         sa[k] = (sums[slot, 6] + other(7)).astype(BF)
         for i in range(3):
-            copy("A", i, k).start()
+            copy("A", i, k, turn).start()
         for b in range(3):
             q = 7 ^ BITS[(b + 2) % 3]
             sums[slot, q - 1] += other(q)
-            for n, (owner, (start, size)) in enumerate(EARLY):
+            for n, (owner, (start, size)) in enumerate(EARLY[turn]):
                 if owner == b:
                     rest = slice(start, start + size)
                     sb[k, b, rest] = sums[slot, q - 1, rest].astype(BF)
-                    copy("E", n, k).start()
+                    copy("E", n, k, turn).start()
         copy("P", 1, k).wait_recv()
         for q in (1, 2, 4):
             sums[slot, q - 1] += other(q)
         mine[k] += other(0)
 
-    def stage_b(k):
+    def stage_b(k, turn):
         slot = lax.rem(k, 3)
         for i in range(3):
-            copy("A", i, k).wait_recv()
+            copy("A", i, k, turn).wait_recv()
             b, q = (i + 1) % 3, 7 ^ BITS[i]
-            part = slice(PARTS[i][0], PARTS[i][0] + PARTS[i][1])
+            start, size = PARTS[(i + turn) % 3]
+            part = slice(start, start + size)
             sb[k, b, part] = (sums[slot, q - 1, part] + ra[k, part].astype(F32)).astype(BF)
-            copy("B", b, k).start()
-
-    def stage_c(k):
+            copy("B", b, k, turn).start()
+
+    def stage_c(k, turn):
         slot = lax.rem(k, 3)
         for i in range(3):
-            for n, (owner, rest) in enumerate(EARLY):
+            for n, (owner, rest) in enumerate(EARLY[turn]):
                 if owner == i:
-                    copy("E", n, k).wait_recv()
-            copy("B", i, k).wait_recv()
+                    copy("E", n, k, turn).wait_recv()
+            copy("B", i, k, turn).wait_recv()
             c = (i + 1) % 3
             sc[k, c] = (sums[slot, BITS[c] - 1] + rb[k, i].astype(F32)).astype(BF)
             copy("C", c, k).start()
@@ -468,37 +478,33 @@
 
     @pl.loop(0, nc + 5)
     def _(t):
+        @pl.when((t > 0) & (t < nc))
+        def _():
+            project(t)
+
+        kb = jnp.where(t <= quick, t - 1, t - 2)
+
+        @pl.when((t >= 1) & (t != quick + 1) & (t < nc + 2))
+        def _():
+            by_turns(kb, stage_b)
+
+        kc = jnp.where(t <= quick + 1, t - 2, t - 3)
+
+        @pl.when((t >= 2) & (t != quick + 2) & (t < nc + 3))
+        def _():
+            by_turns(kc, stage_c)
+
         @pl.when(t < nc)
         def _():
-            project(t)
-
-        kb = jnp.where(t <= quick, t - 1, t - 2)
-
-        @pl.when((t >= 1) & (t != quick + 1) & (t < nc + 2))
-        def _():
-            stage_b(kb)
-
-        kc = jnp.where(t <= quick + 1, t - 2, t - 3)
-
-        @pl.when((t >= 2) & (t != quick + 2) & (t < nc + 3))
-        def _():
-            stage_c(kc)
+            combine(t)
 
         @pl.when(t == 0)
         def _():
-            loads[experts].wait()
+            stage_a(t, 0)
+            loads[experts + 1].wait()
 
         @pl.when(t < nc)
         def _():
-            combine(t)
-
-        @pl.when(t == 0)
-        def _():
-            stage_a(t)
-            loads[experts + 1].wait()
-
-        @pl.when(t < nc)
-        def _():
             shared(t)
 
         @pl.when(t >= 5)
@@ -507,7 +513,7 @@
 
         @pl.when((t > 0) & (t < nc))
         def _():
-            stage_a(t)
+            by_turns(t, stage_a)
 
     @pl.loop(0, nc)
     def _(k):
@@ -516,9 +522,12 @@
             for half in range(2):
                 copy("P", half, k).wait_send()
 
-        for kind, count in (("A", 3), ("B", 3), ("C", 3), ("E", len(EARLY))):
-            for i in range(count):
-                copy(kind, i, k).wait_send()
+        def leave(k, turn):
+            for kind, count in (("A", 3), ("B", 3), ("C", 3), ("E", 4)):
+                for i in range(count):
+                    copy(kind, i, k, turn).wait_send()
+
+        by_turns(k, leave)
 
 
 def solution(mesh):

time: 180 us -> 180 us (level)
  no operation moved by 1% of the time
where the time goes in v4:
time: 180 us
  Pallas kernels  175 us (97%)
  local copies, waits for them, and re-layouts  3.23 us (2%)
    pallas_call x1, Pallas kernels, local(): pl.pallas_call(up_kernel, name='up', out_shape=[jax.ShapeDtypeStruct((exp...  92.8 us
    pallas_call x1, Pallas kernels, local(): pl.pallas_call(down_kernel, name='down', out_shape=jax.ShapeDtypeStruct((...  82.1 us

profile of v4, /device:TPU:0, one launch (start us, length us, event | category | flops | bytes accessed | tf_op | source)
XLA Modules:
  0.0 179.6 jit_solution(16012391211389089269)
XLA Ops:
  0.0 0.1 pad.3.clone
  0.1 0.7 copy.26
  0.8 0.7 fusion.4
  1.5 0.7 maximum_maximum_fusion.m_ref
  2.2 92.8 %up.1 = (bf16[5,384,1536]{2,1,0:T(8,128)(2,1)}, bf16[256,3072]{1,0:T(8,128)(2,1)}, bf16[16,256,128]{2,1,0:T(8,128)(2,1)}) custom-call(bf16[256,2560]{1,0:T(8,128)(2,1)} %bitcast.23, bf16[32,256]{1,0:T(8,128)(2,1)} %maximum_maximum_fusion.m_ref, bf16[5,2560,1536]{2,1,0:T(8,128)(2,1)} %wg.1, bf16[5,2560,1536]{2,1,0:T(8,128)(2,1)} %wu.1, ...), custom_call_target="tpu_custom_call" | custom-call | tf_op jit(solution)/shard_map/up/pallas_call | solution.py:548
  95.0 82.1 %down.1 = bf16[256,2560]{1,0:T(8,128)(2,1)} custom-call(bf16[5,384,1536]{2,1,0:T(8,128)(2,1)} %get-tuple-element.8.h_in, bf16[256,3072]{1,0:T(8,128)(2,1)} %get-tuple-element.9.hs_in, bf16[16,256,128]{2,1,0:T(8,128)(2,1)} %get-tuple-element.10.cm_in, bf16[5,1536,2560]{2,1,0:T(8,128)(2,1)} %wd.1, bf16[3072,2560]{1,0:T(8,128)(2,1)} %sd.1), custom_call_target="tpu_custom_call" | custom-call | tf_op jit(solution)/shard_map/down/pallas_call | solution.py:567
  177.1 2.5 %copy.28 = bf16[1,1,256,2560]{3,2,1,0:T(8,128)(2,1)} copy(bf16[1,1,256,2560]{3,2,1,0:T(8,128)(2,1)} %bitcast.22) | data formatting | bytes 2621440
  (1 shorter events, 0.0 us)
